TPU v7x, 32 devices: a whole 2x2x4 slice. The times are simulated.
32 devices in a mesh: row: 16 (over z, x, core), col: 2 (over y).
Axes of the slice: x: 2, y: 2, z: 4, core: 2. Of those that a mesh axis runs over, the one named last changes fastest.
Arguments:
- species: float32 [2, 128, 128, 64], P(None, None, 'row', 'col'), may hold values from -6 to 6
- symbol_x: float32 [128], replicated, may hold values from 0.3 to 3
- symbol_y: float32 [128], replicated, may hold values from 0.3 to 3
- symbol_z: float32 [64], replicated, may hold values from 0.3 to 3
Outputs:
- spectrum: float32 [2, 128, 128, 64], P(None, 'row', 'col')
All inputs are finite; a program needn't handle non-finite values.
Results may differ from a plain program's by a relative error of at most 0.00007.
Values sent between devices are 32-bit elements; how exact they have to be, the bound alone decides.
A program may use at most 64 MiB of HBM per device.

v0:
```python
import jax
import jax.numpy as jnp
from jax import lax
from jax.sharding import PartitionSpec as P


def basis_table(count):
    rank = jnp.arange(count)
    angle = (
        jnp.pi
        / (4 * count)
        * ((2 * rank[:, None] + 1) * (2 * rank[None, :] + 1) % (8 * count)).astype(jnp.float32)
    )
    return jnp.cos(angle) * (2.0 / count) ** 0.5


def to_modes(values, dim):
    moved = jnp.tensordot(
        values, basis_table(values.shape[dim]), axes=([dim], [0]), precision=lax.Precision.HIGHEST
    )
    return jnp.moveaxis(moved, -1, dim)


def on_device(species, symbol_x, symbol_y, symbol_z):
    part_values = species
    part_values = to_modes(part_values, 1)
    part_values = lax.all_to_all(part_values, "row", split_axis=1, concat_axis=2, tiled=True)
    part_values = to_modes(part_values, 2)
    local_values = part_values
    local_values = lax.all_to_all(local_values, "col", split_axis=2, concat_axis=3, tiled=True)
    local_values = to_modes(local_values, 3)
    share_x = local_values.shape[1]
    part_x = lax.dynamic_slice_in_dim(symbol_x, lax.axis_index("row") * share_x, share_x)
    share_y = local_values.shape[2]
    part_y = lax.dynamic_slice_in_dim(symbol_y, lax.axis_index("col") * share_y, share_y)
    symbol = part_x[:, None, None] + part_y[None, :, None] + symbol_z[None, None, :]
    local_values = local_values / symbol
    return local_values


def solution(mesh):
    in_specs = (P(None, None, "row", "col"), P(), P(), P())
    out_specs = P(None, "row", "col", None)
    return jax.shard_map(
        on_device, mesh=mesh, in_specs=in_specs, out_specs=out_specs, check_vma=False
    )
```

profile of v0, /device:TPU:0, one launch (start us, length us, event | category | flops | bytes accessed | tf_op | source)
XLA Modules:
  0.0 39.9 jit_solution(311103156641426891)
XLA Ops:
  0.0 0.0 copy-start
  0.0 0.9 %copy-done = f32[2,128,8,32]{1,3,2,0:T(8,128)S(1)} copy-done((f32[2,128,8,32]{1,3,2,0:T(8,128)S(1)}, f32[2,128,8,32]{1,3,2,0:T(8,128)}, u32[]{:S(2)}) %copy-start) | copy-done | bytes 262168
  1.0 0.7 %fusion.16 = f32[128,512]{0,1:S(1)} fusion(f32[128,512]{0,1:T(8,128)S(1)} %bitcast.33, s32[128]{0:T(128)S(1)} %multiply_add_fusion.1), kind=kOutput, calls=%fused_computation.27 | convolution fusion | flops 100909056 | bytes 524800
  1.6 0.5 %copy.18 = f32[2,128,8,32]{3,2,0,1:T(8,128)S(1)} copy(f32[2,128,8,32]{1,3,2,0:T(8,128)S(1)} %bitcast.39) | data formatting | bytes 524288 | tf_op jit(solution)/shard_map/transpose | solution.py:21
  2.1 1.2 %reshape.66 = f32[16,1,4096]{2,1,0:T(1,128)} reshape(f32[128,2,8,32]{3,2,1,0:T(8,128)S(1)} %bitcast.34) | data formatting | bytes 524288
  3.3 7.4 %all-to-all-start = ((f32[16,1,4096]{2,1,0:T(1,128)}), f32[16,1,4096]{2,1,0:T(1,128)S(1)}, u32[]{:S(2)}, u32[]{:S(2)}) async-start(f32[16,1,4096]{2,1,0:T(1,128)} %reshape.66), calls=%async_computation | async-start | bytes 524288 | tf_op jit(solution)/shard_map/all_to_all | solution.py:27
  10.7 0.0 copy-start.2
  10.7 0.6 %copy-done.2 = f32[128]{0:T(128)S(1)} copy-done((f32[128]{0:T(128)S(1)}, f32[128]{0:T(128)}, u32[]{:S(2)}) %copy-start.2) | copy-done | bytes 536
  11.4 0.1 dynamic_slice.7
  11.4 0.0 copy-start.3
  11.4 0.7 %copy-done.3 = f32[128]{0:T(128)S(1)} copy-done((f32[128]{0:T(128)S(1)}, f32[128]{0:T(128)}, u32[]{:S(2)}) %copy-start.3) | copy-done | bytes 536
  12.1 0.1 dynamic_slice.6
  12.2 0.1 broadcast_add_fusion.1
  12.2 8.5 %all-to-all-done = f32[16,1,4096]{2,1,0:T(1,128)S(1)} async-done(((f32[16,1,4096]{2,1,0:T(1,128)}), f32[16,1,4096]{2,1,0:T(1,128)S(1)}, u32[]{:S(2)}, u32[]{:S(2)}) %all-to-all-start) | async-done | bytes 262176 | tf_op jit(solution)/shard_map/all_to_all | solution.py:27
  20.7 0.6 %broadcast.126 = f32[]{:T(128)} broadcast(f32[]{:T(128)} %constant.114), dimensions={} | broadcast | bytes 8 | tf_op jit(solution)/shard_map/all_to_all | solution.py:27
  21.3 1.2 %reduce = f32[16,4096]{1,0:T(8,128)S(1)} reduce(f32[16,1,4096]{2,1,0:T(1,128)S(1)} %all-to-all-done, f32[]{:T(128)} %broadcast.126), dimensions={1}, to_apply=%all_to_all.26.reduce_sub_computation | reduce | bytes 524292 | tf_op jit(solution)/shard_map/all_to_all | solution.py:27
  22.5 0.3 reshape.67
  22.9 1.9 %convolution_bitcast_fusion = f32[2,8,128,32]{2,3,1,0:T(8,128)S(1)} fusion(f32[2,8,16,8,32]{4,3,0,1,2:T(8,128)S(1)} %bitcast.37, s32[128]{0:T(128)S(1)} %multiply_add_fusion.1), kind=kOutput, calls=%fused_computation.1 | convolution fusion | flops 100909056 | bytes 524800 | tf_op jit(solution)/shard_map/dot_general | solution.py:18
  24.8 0.5 %copy.22 = f32[2,8,128,32]{3,1,0,2:T(8,128)S(1)} copy(f32[2,8,128,32]{2,3,1,0:T(8,128)S(1)} %convolution_bitcast_fusion) | data formatting | bytes 524288 | tf_op jit(solution)/shard_map/transpose | solution.py:21
  25.3 1.2 %reshape.68 = f32[2,1,32768]{2,1,0:T(1,128)} reshape(f32[128,2,8,32]{3,2,1,0:T(8,128)S(1)} %bitcast.35) | data formatting | bytes 524288
  26.5 0.0 copy-start.1
  26.5 3.6 %all-to-all-start.1 = ((f32[2,1,32768]{2,1,0:T(1,128)}), f32[2,1,32768]{2,1,0:T(1,128)S(1)}, u32[]{:S(2)}, u32[]{:S(2)}) async-start(f32[2,1,32768]{2,1,0:T(1,128)} %reshape.68), calls=%async_computation.1 | async-start | bytes 524288 | tf_op jit(solution)/shard_map/all_to_all | solution.py:30
  30.1 0.0 copy-done.1
  30.1 0.1 broadcast_add_fusion
  30.2 5.3 %all-to-all-done.1 = f32[2,1,32768]{2,1,0:T(1,128)S(1)} async-done(((f32[2,1,32768]{2,1,0:T(1,128)}), f32[2,1,32768]{2,1,0:T(1,128)S(1)}, u32[]{:S(2)}, u32[]{:S(2)}) %all-to-all-start.1) | async-done | bytes 262176 | tf_op jit(solution)/shard_map/all_to_all | solution.py:30
  35.6 1.4 %reduce.1 = f32[2,32768]{1,0:T(2,128)S(1)} reduce(f32[2,1,32768]{2,1,0:T(1,128)S(1)} %all-to-all-done.1, f32[]{:T(128)} %broadcast.126), dimensions={1}, to_apply=%all_to_all.30.reduce_sub_computation | reduce | bytes 524292 | tf_op jit(solution)/shard_map/all_to_all | solution.py:30
  37.0 0.5 %reshape.69 = f32[128,2,8,32]{3,2,1,0:T(8,128)S(1)} reshape(f32[2,32768]{1,0:T(2,128)S(1)} %reduce.1) | data formatting | bytes 524288
  37.5 0.5 %copy.31 = f32[2,8,2,64,32]{3,2,4,1,0:T(2,128)S(1)} copy(f32[2,8,2,64,32]{4,1,0,3,2:T(8,128)S(1)} %bitcast.36) | data formatting | bytes 524288 | tf_op jit(solution)/shard_map/all_to_all | solution.py:30
  38.0 0.1 copy.24
  38.0 1.8 %convolution_divide_fusion = f32[2,8,64,64]{3,2,1,0:T(8,128)} fusion(f32[2,8,64,64]{2,3,1,0:T(8,128)S(1)} %bitcast.40, f32[8,64,64]{2,1,0:T(8,128)S(1)} %broadcast_add_fusion, s32[64]{0:T(128)S(1)} %multiply_add_fusion), kind=kOutput, calls=%fused_computation | convolution fusion | flops 50458624 | bytes 655616 | tf_op jit(solution)/shard_map/dot_general | solution.py:18
  (2 shorter events, 0.0 us)
Async XLA Ops:
  0.0 1.0 %copy-start = (f32[2,128,8,32]{1,3,2,0:T(8,128)S(1)}, f32[2,128,8,32]{1,3,2,0:T(8,128)}, u32[]{:S(2)}) copy-start(f32[2,128,8,32]{1,3,2,0:T(8,128)} %param.4) | copy-start | bytes 786436
  3.3 17.4 %all-to-all-start = ((f32[16,1,4096]{2,1,0:T(1,128)}), f32[16,1,4096]{2,1,0:T(1,128)S(1)}, u32[]{:S(2)}, u32[]{:S(2)}) async-start(f32[16,1,4096]{2,1,0:T(1,128)} %reshape.66), calls=%async_computation | async-start | bytes 524288 | tf_op jit(solution)/shard_map/all_to_all | solution.py:27
  10.7 0.7 %copy-start.2 = (f32[128]{0:T(128)S(1)}, f32[128]{0:T(128)}, u32[]{:S(2)}) copy-start(f32[128]{0:T(128)} %param.6) | copy-start | bytes 1540
  11.4 0.7 %copy-start.3 = (f32[128]{0:T(128)S(1)}, f32[128]{0:T(128)}, u32[]{:S(2)}) copy-start(f32[128]{0:T(128)} %param.5) | copy-start | bytes 1540
  26.5 3.6 %copy-start.1 = (f32[64]{0:T(128)S(1)}, f32[64]{0:T(128)}, u32[]{:S(2)}) copy-start(f32[64]{0:T(128)} %param.7) | copy-start | bytes 772
  26.5 9.1 %all-to-all-start.1 = ((f32[2,1,32768]{2,1,0:T(1,128)}), f32[2,1,32768]{2,1,0:T(1,128)S(1)}, u32[]{:S(2)}, u32[]{:S(2)}) async-start(f32[2,1,32768]{2,1,0:T(1,128)} %reshape.68), calls=%async_computation.1 | async-start | bytes 524288 | tf_op jit(solution)/shard_map/all_to_all | solution.py:30
where the time goes:
time: 40.2 us; the launch traced here: 39.9 us
  waiting for transfers between devices  13.8 us (34%)
  starting transfers between devices  11 us (27%)
  local copies, waits for them, and re-layouts  7.65 us (19%)
  matrix products  4.44 us (11%)
  other arithmetic  2.88 us (7%)
    all_to_all x1, waiting for transfers between devices, on_device(): lax.all_to_all(part_values, 'row', split_axis=1, concat_axis=2, tiled=True)  8.47 us
    all_to_all x1, starting transfers between devices, on_device(): lax.all_to_all(part_values, 'row', split_axis=1, concat_axis=2, tiled=True)  7.39 us
    unnamed x12, local copies, waits for them, and re-layouts  5.37 us
    all_to_all x1, waiting for transfers between devices, on_device(): lax.all_to_all(local_values, 'col', split_axis=2, concat_axis=3, tiled=True)  5.35 us
    dot_general x2, matrix products, to_modes(): jnp.tensordot(values, basis_table(values.shape[dim]), axes=([dim], [0]),...  3.76 us
    all_to_all x1, starting transfers between devices, on_device(): lax.all_to_all(local_values, 'col', split_axis=2, concat_axis=3, tiled=True)  3.58 us
    all_to_all x1, other arithmetic, on_device(): lax.all_to_all(local_values, 'col', split_axis=2, concat_axis=3, tiled=True)  1.43 us
    all_to_all x1, other arithmetic, on_device(): lax.all_to_all(part_values, 'row', split_axis=1, concat_axis=2, tiled=True)  1.25 us
  transfers between devices with their start and end apart: 2, of which 2 were waited for; matrix products, arithmetic and copies ran while one was open for 1% of the time, Pallas kernels for 0%

commit v1 on v0

v1 whole, which is shorter than its diff:
```python
import functools

import jax
import jax.numpy as jnp
import ml_dtypes
import numpy as np
from jax import lax
from jax.experimental import pallas as pl
from jax.experimental.pallas import tpu as pltpu
from jax.sharding import PartitionSpec as P

LANES = 128
CUTS = 2
F32, BF16 = jnp.float32, jnp.bfloat16


def basis_table(count):
    odd = 2 * np.arange(count) + 1
    angle = np.pi / (4 * count) * (odd[:, None] * odd[None, :] % (8 * count))
    return np.cos(angle) * (2.0 / count) ** 0.5


def halves(table):
    high = table.astype(ml_dtypes.bfloat16)
    low = (table - high.astype(np.float64)).astype(ml_dtypes.bfloat16)
    return high, low


def split(values):
    high = values.astype(BF16)
    low = (values - high.astype(F32)).astype(BF16)
    return high, low


def tables(nx, ny, nz, share_z):
    width = LANES // share_z
    lane = np.arange(nx)
    group, rest = lane // LANES, lane % LANES
    order = width * (group * share_z + rest % share_z) + rest // share_z
    high, low = halves(basis_table(nx)[:, order])
    table_x = np.block([[high, low], [high, low]])
    high, low = halves(basis_table(ny))
    table_y = np.block([[high, high], [low, low]])
    eye = np.eye(width)
    wide = np.concatenate(
        [np.kron(eye, part) for part in np.split(basis_table(nz), nz // share_z, axis=0)], axis=0
    )
    table_z = np.stack(halves(wide))
    return table_x, table_y, table_z


def kernel(
    rows, cols, names,
    species, hx_hbm, hy_hbm, wz_hbm, sx_hbm, sy_hbm, sz_hbm,
    out,
    xin, hx, hy, wz, sx, sy, sz, send, recv, mixed, lines, tall_x, tall_y, scale,
    in_sem, row_send, row_recv, col_send, col_recv,
):
    row_name, col_name = names
    fields, share_y, share_z, nx = species.shape
    ny = rows * share_y
    nz = sz.shape[1]
    share_x, half_y = nx // rows, ny // cols
    width = LANES // share_z
    quads = share_x // width
    wide = quads * LANES // CUTS
    me, my_col = lax.axis_index(row_name), lax.axis_index(col_name)

    barrier = pltpu.get_barrier_semaphore()
    for k in range(1, rows):
        pl.semaphore_signal(
            barrier, inc=1, device_id={row_name: (me + k) % rows},
            device_id_type=pl.DeviceIdType.MESH,
        )
    for k in range(1, cols):
        pl.semaphore_signal(
            barrier, inc=1, device_id={col_name: (my_col + k) % cols},
            device_id_type=pl.DeviceIdType.MESH,
        )

    loads = [pltpu.make_async_copy(species.at[f], xin.at[f], in_sem.at[f]) for f in range(fields)]
    pairs = ((hx_hbm, hx), (hy_hbm, hy), (wz_hbm, wz), (sx_hbm, sx), (sy_hbm, sy), (sz_hbm, sz))
    fetches = [
        pltpu.make_async_copy(a, b, in_sem.at[fields + i]) for i, (a, b) in enumerate(pairs)
    ]
    loads[0].start()
    fetches[0].start()
    for copy in loads[1:] + fetches[1:]:
        copy.start()

    lane = lax.broadcasted_iota(jnp.int32, (share_y, LANES), 1)
    order = sorted(range(1, rows), key=lambda k: -min(k, rows - k))

    def row_copy(piece, target, origin):
        return pltpu.make_async_remote_copy(
            src_ref=send.at[piece, target],
            dst_ref=recv.at[piece, origin],
            send_sem=row_send.at[piece, target],
            recv_sem=row_recv.at[piece, origin],
            device_id={row_name: target},
            device_id_type=pl.DeviceIdType.MESH,
        )

    def col_copy(piece, target, origin):
        return pltpu.make_async_remote_copy(
            src_ref=mixed.at[piece, target],
            dst_ref=lines.at[piece, origin],
            send_sem=col_send.at[piece, target],
            recv_sem=col_recv.at[piece, origin],
            device_id={col_name: target},
            device_id_type=pl.DeviceIdType.MESH,
        )

    for f in range(fields):
        loads[f].wait()
        if f == 0:
            fetches[0].wait()
        high, low = split(
            jnp.concatenate(
                [xin[f, :, z, :] for z in range(share_z)], axis=0
            )
        )
        both = jnp.dot(
            jnp.concatenate([high, low], axis=1), hx[...], preferred_element_type=F32
        )
        both = both[:, :nx] + both[:, nx:]
        for group in range(nx // LANES):
            tiles = [
                both[z * share_y : (z + 1) * share_y, group * LANES : (group + 1) * LANES]
                for z in range(share_z)
            ]
            bit = 1
            while bit < share_z:
                keep = (lane & bit) == 0
                for i in range(share_z):
                    if i & bit == 0:
                        a, b = tiles[i], tiles[i + bit]
                        tiles[i] = jnp.where(keep, a, pltpu.roll(b, bit, 1))
                        tiles[i + bit] = jnp.where(keep, pltpu.roll(a, LANES - bit, 1), b)
                bit *= 2
            for i in range(share_z):
                q = group * share_z + i
                target, at = q // quads, q % quads * LANES
                send[f * CUTS + at // wide, target, :, at % wide : at % wide + LANES] = tiles[i]
        if f == 0:
            pl.semaphore_wait(barrier, rows + cols - 2)
        for cut in range(CUTS):
            piece = f * CUTS + cut
            for k in order:
                row_copy(piece, (me + k) % rows, me).start()
            recv[piece, me] = send[piece, me]

    for copy in fetches[1:]:
        copy.wait()
    tall_x[...] = jnp.broadcast_to(sx[...], (LANES, nx)).T
    tall_y[...] = jnp.broadcast_to(sy[...], (LANES, ny)).T
    part_y = tall_y[pl.ds(my_col * half_y, half_y), :1]
    for x in range(share_x):
        part_x = tall_x[pl.ds(me * share_x + x, 1), :1]
        at = x % width * nz
        scale[x // width, :, at : at + nz] = 1.0 / (part_x + part_y + sz[...])

    for piece in range(fields * CUTS):
        for k in order:
            origin = (me + rows - k) % rows
            row_copy(piece, origin, origin).wait_recv()
        high, low = split(recv[piece].reshape(ny, wide))
        both = jnp.dot(
            hy[...], jnp.concatenate([high, low], axis=0), preferred_element_type=F32
        )
        both = both[:ny] + both[ny:]
        mixed[piece] = both.reshape(cols, half_y, wide)
        for k in range(1, cols):
            col_copy(piece, (my_col + k) % cols, my_col).start()
        lines[piece, my_col] = mixed[piece, my_col]

    for piece in range(fields * CUTS):
        for k in range(1, cols):
            origin = (my_col + cols - k) % cols
            col_copy(piece, origin, origin).wait_recv()
        f, cut = piece // CUTS, piece % CUTS
        for i in range(wide // LANES):
            quad = cut * (wide // LANES) + i
            line = jnp.concatenate(
                [lines[piece, c, :, i * LANES : (i + 1) * LANES] for c in range(cols)], axis=1
            )
            high, low = split(line)
            both = jnp.dot(
                jnp.concatenate([high, low], axis=0), wz[0], preferred_element_type=F32
            )
            done = both[:half_y] + both[half_y:]
            done = done + jnp.dot(high, wz[1], preferred_element_type=F32)
            done = done * scale[quad]
            for j in range(width):
                out[f, quad * width + j] = done[:, j * nz : (j + 1) * nz]

    for piece in range(fields * CUTS):
        for k in order:
            row_copy(piece, (me + k) % rows, me).wait_send()
        for k in range(1, cols):
            col_copy(piece, (my_col + k) % cols, my_col).wait_send()


def on_device(rows, cols, species, symbol_x, symbol_y, symbol_z):
    fields, nx, share_y, share_z = species.shape
    ny, nz = symbol_y.shape[0], symbol_z.shape[0]
    share_x, half_y = nx // rows, ny // cols
    width = LANES // share_z
    pieces, wide = fields * CUTS, share_x // width * LANES // CUTS
    hx, hy, wz = (jnp.asarray(t) for t in tables(nx, ny, nz, share_z))
    dma = pltpu.SemaphoreType.DMA
    return pl.pallas_call(
        functools.partial(kernel, rows, cols, ("row", "col")),
        out_shape=jax.ShapeDtypeStruct((fields, share_x, half_y, nz), F32),
        in_specs=[pl.BlockSpec(memory_space=pl.ANY)] * 7,
        out_specs=pl.BlockSpec(memory_space=pltpu.VMEM),
        scratch_shapes=[
            pltpu.VMEM((fields, share_y, share_z, nx), F32),
            pltpu.VMEM(hx.shape, BF16),
            pltpu.VMEM(hy.shape, BF16),
            pltpu.VMEM(wz.shape, BF16),
            pltpu.VMEM((1, nx), F32),
            pltpu.VMEM((1, ny), F32),
            pltpu.VMEM((1, nz), F32),
            pltpu.VMEM((pieces, rows, share_y, wide), F32),
            pltpu.VMEM((pieces, rows, share_y, wide), F32),
            pltpu.VMEM((pieces, cols, half_y, wide), F32),
            pltpu.VMEM((pieces, cols, half_y, wide), F32),
            pltpu.VMEM((nx, LANES), F32),
            pltpu.VMEM((ny, LANES), F32),
            pltpu.VMEM((share_x // width, half_y, width * nz), F32),
            dma((fields + 6,)),
            dma((pieces, rows)),
            dma((pieces, rows)),
            dma((pieces, cols)),
            dma((pieces, cols)),
        ],
        compiler_params=pltpu.CompilerParams(collective_id=0, has_side_effects=True),
    )(
        jnp.transpose(species, (0, 2, 3, 1)), hx, hy, wz,
        symbol_x[None, :], symbol_y[None, :], symbol_z[None, :],
    )


def solution(mesh):
    rows, cols = mesh.shape["row"], mesh.shape["col"]
    in_specs = (P(None, None, "row", "col"), P(), P(), P())
    out_specs = P(None, "row", "col", None)
    return jax.shard_map(
        functools.partial(on_device, rows, cols),
        mesh=mesh, in_specs=in_specs, out_specs=out_specs, check_vma=False,
    )
```

time: 40.2 us -> 21.2 us (0.53)
  Pallas kernels: 0 us -> 19.2 us
  waiting for transfers between devices: 13.8 us -> 0 us
  starting transfers between devices: 11 us -> 0 us
  local copies, waits for them, and re-layouts: 7.65 us -> 1.89 us
  matrix products: 4.44 us -> 0 us
  other arithmetic: 2.88 us -> 0 us
    pallas_call x0 -> x1, Pallas kernels: none -> 19.2 us  [on_device(): pl.pallas_call(functools.partial(kernel, rows, cols, ('row', 'col')), out...]
    all_to_all x2 -> x0, waiting for transfers between devices: 13.8 us -> none  [the longest x1 8.47 us: on_device(): lax.all_to_all(part_values, 'row', split_axis=1, concat_axis=2, tiled=True)]
    all_to_all x2 -> x0, starting transfers between devices: 11 us -> none  [the longest x1 7.39 us: on_device(): lax.all_to_all(part_values, 'row', split_axis=1, concat_axis=2, tiled=True)]
    dot_general x2 -> x0, matrix products: 3.76 us -> none  [to_modes(): jnp.tensordot(values, basis_table(values.shape[dim]), axes=([dim], [0]),...]
    unnamed x12 -> x1, local copies, waits for them, and re-layouts: 5.37 us -> 1.89 us
    all_to_all x2 -> x0, other arithmetic: 2.67 us -> none  [the longest x1 1.43 us: on_device(): lax.all_to_all(local_values, 'col', split_axis=2, concat_axis=3, tiled=True)]
    all_to_all x3 -> x0, local copies, waits for them, and re-layouts: 1.14 us -> none  [the longest x1 0.57 us: on_device(): lax.all_to_all(part_values, 'row', split_axis=1, concat_axis=2, tiled=True)]
    transpose x2 -> x0, local copies, waits for them, and re-layouts: 0.99 us -> none  [to_modes(): return jnp.moveaxis(moved, -1, dim)]
  transfers between devices with their start and end apart: 2 -> 0, of which waited for: 2 -> 0; matrix products, arithmetic and copies ran while one was open for 1% -> 0% of each run, Pallas kernels for 0% -> 0%
where the time goes in v1:
time: 21.2 us; the launch traced here: 21.1 us
  Pallas kernels  19.2 us (91%)
  local copies, waits for them, and re-layouts  1.89 us (9%)
    pallas_call x1, Pallas kernels, on_device(): pl.pallas_call(functools.partial(kernel, rows, cols, ('row', 'col')), out...  19.2 us
    unnamed x1, local copies, waits for them, and re-layouts  1.89 us

profile of v1, /device:TPU:0, one launch (start us, length us, event | category | flops | bytes accessed | tf_op | source)
XLA Modules:
  0.0 21.1 jit_solution(14734036016026168427)
XLA Ops:
  0.0 19.2 %shard_map.73 = f32[2,8,64,64]{3,2,1,0:T(8,128)} custom-call(f32[2,8,32,128]{3,2,1,0:T(8,128)} %bitcast.4, bf16[256,256]{1,0:T(8,128)(2,1)} %constant.6.clone.hx_hbm, bf16[256,256]{1,0:T(8,128)(2,1)} %constant.7.clone.hy_hbm, bf16[2,256,256]{2,1,0:T(8,128)(2,1)} %constant.8.clone.wz_hbm, f32[1,128]{1,0:T(1,128)} %bitcast.5, f32[1,128]{1,0:T(1,128)} %bitcast.6, ...), custom_call_target="tpu_custom_call" | custom-call | tf_op jit(solution)/shard_map/pallas_call | solution.py:212
  19.2 1.9 %copy.9 = f32[2,8,64,64]{3,2,1,0:T(8,128)} copy(f32[2,8,64,64]{3,2,1,0:T(8,128)} %shard_map.73) | data formatting | bytes 524288

commit v2 on v1

--- a/solution.py
+++ b/solution.py
@@ -10,7 +10,7 @@
 from jax.sharding import PartitionSpec as P
 
 LANES = 128
-CUTS = 2
+CUTS = 1
 F32, BF16 = jnp.float32, jnp.bfloat16
 
 
@@ -51,9 +51,9 @@
 
 def kernel(
     rows, cols, names,
-    species, hx_hbm, hy_hbm, wz_hbm, sx_hbm, sy_hbm, sz_hbm,
-    out,
-    xin, hx, hy, wz, sx, sy, sz, send, recv, mixed, lines, tall_x, tall_y, scale,
+    species, hx_hbm, hy_hbm, sx_hbm, sy_hbm, sz_hbm,
+    lines, scale,
+    xin, hx, hy, sx, sy, sz, send, recv, mixed, tall_x, tall_y,
     in_sem, row_send, row_recv, col_send, col_recv,
 ):
     row_name, col_name = names
@@ -79,7 +79,7 @@
         )
 
     loads = [pltpu.make_async_copy(species.at[f], xin.at[f], in_sem.at[f]) for f in range(fields)]
-    pairs = ((hx_hbm, hx), (hy_hbm, hy), (wz_hbm, wz), (sx_hbm, sx), (sy_hbm, sy), (sz_hbm, sz))
+    pairs = ((hx_hbm, hx), (hy_hbm, hy), (sx_hbm, sx), (sy_hbm, sy), (sz_hbm, sz))
     fetches = [
         pltpu.make_async_copy(a, b, in_sem.at[fields + i]) for i, (a, b) in enumerate(pairs)
     ]
@@ -175,9 +175,20 @@
         lines[piece, my_col] = mixed[piece, my_col]
 
     for piece in range(fields * CUTS):
+        for k in order:
+            row_copy(piece, (me + k) % rows, me).wait_send()
         for k in range(1, cols):
             origin = (my_col + cols - k) % cols
             col_copy(piece, origin, origin).wait_recv()
+            col_copy(piece, (my_col + k) % cols, my_col).wait_send()
+
+
+def last_kernel(lines, scale, wz, out, held, out_sem):
+    pieces, cols, half_y, wide = lines.shape
+    nz = out.shape[3]
+    width = scale.shape[2] // nz
+    copies = []
+    for piece in range(pieces):
         f, cut = piece // CUTS, piece % CUTS
         for i in range(wide // LANES):
             quad = cut * (wide // LANES) + i
@@ -192,13 +203,13 @@
             done = done + jnp.dot(high, wz[1], preferred_element_type=F32)
             done = done * scale[quad]
             for j in range(width):
-                out[f, quad * width + j] = done[:, j * nz : (j + 1) * nz]
-
-    for piece in range(fields * CUTS):
-        for k in order:
-            row_copy(piece, (me + k) % rows, me).wait_send()
-        for k in range(1, cols):
-            col_copy(piece, (my_col + k) % cols, my_col).wait_send()
+                held[f, quad * width + j] = done[:, j * nz : (j + 1) * nz]
+            span = pl.ds(quad * width, width)
+            copy = pltpu.make_async_copy(held.at[f, span], out.at[f, span], out_sem.at[f, quad])
+            copy.start()
+            copies.append(copy)
+    for copy in copies:
+        copy.wait()
 
 
 def on_device(rows, cols, species, symbol_x, symbol_y, symbol_z):
@@ -209,37 +220,48 @@
     pieces, wide = fields * CUTS, share_x // width * LANES // CUTS
     hx, hy, wz = (jnp.asarray(t) for t in tables(nx, ny, nz, share_z))
     dma = pltpu.SemaphoreType.DMA
-    return pl.pallas_call(
+    width_z = width * nz
+    vmem = pl.BlockSpec(memory_space=pltpu.VMEM)
+    lines, scale = pl.pallas_call(
         functools.partial(kernel, rows, cols, ("row", "col")),
-        out_shape=jax.ShapeDtypeStruct((fields, share_x, half_y, nz), F32),
-        in_specs=[pl.BlockSpec(memory_space=pl.ANY)] * 7,
-        out_specs=pl.BlockSpec(memory_space=pltpu.VMEM),
+        out_shape=(
+            jax.ShapeDtypeStruct((pieces, cols, half_y, wide), F32),
+            jax.ShapeDtypeStruct((share_x // width, half_y, width_z), F32),
+        ),
+        in_specs=[pl.BlockSpec(memory_space=pl.ANY)] * 6,
+        out_specs=(vmem, vmem),
         scratch_shapes=[
             pltpu.VMEM((fields, share_y, share_z, nx), F32),
             pltpu.VMEM(hx.shape, BF16),
             pltpu.VMEM(hy.shape, BF16),
-            pltpu.VMEM(wz.shape, BF16),
             pltpu.VMEM((1, nx), F32),
             pltpu.VMEM((1, ny), F32),
             pltpu.VMEM((1, nz), F32),
             pltpu.VMEM((pieces, rows, share_y, wide), F32),
             pltpu.VMEM((pieces, rows, share_y, wide), F32),
             pltpu.VMEM((pieces, cols, half_y, wide), F32),
-            pltpu.VMEM((pieces, cols, half_y, wide), F32),
             pltpu.VMEM((nx, LANES), F32),
             pltpu.VMEM((ny, LANES), F32),
-            pltpu.VMEM((share_x // width, half_y, width * nz), F32),
-            dma((fields + 6,)),
+            dma((fields + 5,)),
             dma((pieces, rows)),
             dma((pieces, rows)),
             dma((pieces, cols)),
             dma((pieces, cols)),
         ],
-        compiler_params=pltpu.CompilerParams(collective_id=0, has_side_effects=True),
+        compiler_params=pltpu.CompilerParams(collective_id=0, has_side_effects=True, vmem_limit_bytes=16 * 2**20),
     )(
-        jnp.transpose(species, (0, 2, 3, 1)), hx, hy, wz,
-        symbol_x[None, :], symbol_y[None, :], symbol_z[None, :],
+        *(pltpu.with_memory_space_constraint(v, pltpu.HBM) for v in (jnp.transpose(species, (0, 2, 3, 1)), hx, hy,
+        symbol_x[None, :], symbol_y[None, :], symbol_z[None, :])),
     )
+    shape = (fields, share_x, half_y, nz)
+    return pl.pallas_call(
+        last_kernel,
+        out_shape=jax.ShapeDtypeStruct(shape, F32),
+        in_specs=[vmem, vmem, vmem],
+        out_specs=pl.BlockSpec(memory_space=pl.ANY),
+        scratch_shapes=[pltpu.VMEM(shape, F32), dma((fields, share_x // width))],
+        compiler_params=pltpu.CompilerParams(vmem_limit_bytes=16 * 2**20),
+    )(lines, scale, wz)
 
 
 def solution(mesh):

time: 21.2 us -> 18.9 us (0.89)
  local copies, waits for them, and re-layouts: 1.89 us -> 0.01 us
  Pallas kernels: 19.2 us -> 18.7 us
    unnamed x1 -> x2, local copies, waits for them, and re-layouts: 1.89 us -> 0.01 us
    pallas_call x1, Pallas kernels: 19.2 us -> 17.6 us  [on_device(): pl.pallas_call(functools.partial(kernel, rows, cols, ('row', 'col')), out...]
    pallas_call x0 -> x1, Pallas kernels: none -> 1.14 us  [on_device(): pl.pallas_call(last_kernel, out_shape=jax.ShapeDtypeStruct(shape, F32), i...]
where the time goes in v2:
time: 18.9 us; the launch traced here: 18.7 us
  Pallas kernels  18.7 us (99%)
    pallas_call x1, Pallas kernels, on_device(): pl.pallas_call(functools.partial(kernel, rows, cols, ('row', 'col')), out...  17.6 us
    pallas_call x1, Pallas kernels, on_device(): pl.pallas_call(last_kernel, out_shape=jax.ShapeDtypeStruct(shape, F32), i...  1.14 us

profile of v2, /device:TPU:0, one launch (start us, length us, event | category | flops | bytes accessed | tf_op | source)
XLA Modules:
  0.0 18.7 jit_solution(13972454074693541848)
XLA Ops:
  0.0 0.0 copy-start
  0.0 17.6 %shard_map.73 = (f32[2,2,64,256]{3,2,1,0:T(8,128)S(1)}, f32[2,64,256]{2,1,0:T(8,128)S(1)}) custom-call(f32[2,8,32,128]{3,2,1,0:T(8,128)} %bitcast.4, bf16[256,256]{1,0:T(8,128)(2,1)} %constant.6.clone.hx_hbm, bf16[256,256]{1,0:T(8,128)(2,1)} %constant.7.clone.hy_hbm, f32[1,128]{1,0:T(1,128)} %bitcast.5, f32[1,128]{1,0:T(1,128)} %bitcast.6, f32[1,64]{1,0:T(1,128)} %bitcast.7), custom_call_target="tpu_custom_call" | custom-call | tf_op jit(solution)/shard_map/pallas_call | solution.py:225
  17.6 0.0 copy-done
  17.6 1.1 %shard_map.74 = f32[2,8,64,64]{3,2,1,0:T(8,128)} custom-call(f32[2,2,64,256]{3,2,1,0:T(8,128)S(1)} %get-tuple-element.7.lines, f32[2,64,256]{2,1,0:T(8,128)S(1)} %get-tuple-element.8.scale, bf16[2,256,256]{2,1,0:T(8,128)(2,1)S(1)} %copy-done), custom_call_target="tpu_custom_call" | custom-call | tf_op jit(solution)/shard_map/pallas_call | solution.py:257
Async XLA Ops:
  0.0 17.6 %copy-start = (bf16[2,256,256]{2,1,0:T(8,128)(2,1)S(1)}, bf16[2,256,256]{2,1,0:T(8,128)(2,1)}, u32[]{:S(2)}) copy-start(bf16[2,256,256]{2,1,0:T(8,128)(2,1)} %constant.8.clone.wz) | copy-start | bytes 786436

commit v3 on v2

--- a/solution.py
+++ b/solution.py
@@ -38,7 +38,7 @@
     group, rest = lane // LANES, lane % LANES
     order = width * (group * share_z + rest % share_z) + rest // share_z
     high, low = halves(basis_table(nx)[:, order])
-    table_x = np.block([[high, low], [high, low]])
+    table_x = np.concatenate([high, low], axis=1)
     high, low = halves(basis_table(ny))
     table_y = np.block([[high, high], [low, low]])
     eye = np.eye(width)
@@ -85,7 +85,7 @@
     ]
     loads[0].start()
     fetches[0].start()
-    for copy in loads[1:] + fetches[1:]:
+    for copy in loads[1:]:
         copy.start()
 
     lane = lax.broadcasted_iota(jnp.int32, (share_y, LANES), 1)
@@ -120,8 +120,9 @@
                 [xin[f, :, z, :] for z in range(share_z)], axis=0
             )
         )
+        table = jnp.concatenate([hx[...], hx[...]], axis=0)
         both = jnp.dot(
-            jnp.concatenate([high, low], axis=1), hx[...], preferred_element_type=F32
+            jnp.concatenate([high, low], axis=1), table, preferred_element_type=F32
         )
         both = both[:, :nx] + both[:, nx:]
         for group in range(nx // LANES):
@@ -148,8 +149,11 @@
             piece = f * CUTS + cut
             for k in order:
                 row_copy(piece, (me + k) % rows, me).start()
-            recv[piece, me] = send[piece, me]
-
+
+    for copy in fetches[1:]:
+        copy.start()
+    for piece in range(fields * CUTS):
+        recv[piece, me] = send[piece, me]
     for copy in fetches[1:]:
         copy.wait()
     tall_x[...] = jnp.broadcast_to(sx[...], (LANES, nx)).T

time: 18.9 us -> 18.9 us (level)
  no operation moved by 1% of the time
where the time goes in v3:
time: 18.9 us; the launch traced here: 18.7 us
  Pallas kernels  18.7 us (99%)
    pallas_call x1, Pallas kernels, on_device(): pl.pallas_call(functools.partial(kernel, rows, cols, ('row', 'col')), out...  17.6 us
    pallas_call x1, Pallas kernels, on_device(): pl.pallas_call(last_kernel, out_shape=jax.ShapeDtypeStruct(shape, F32), i...  1.14 us

profile of v3, /device:TPU:0, one launch (start us, length us, event | category | flops | bytes accessed | tf_op | source)
XLA Modules:
  0.0 18.7 jit_solution(18108351467017008869)
XLA Ops:
  0.0 0.0 copy-start
  0.0 17.6 %shard_map.73 = (f32[2,2,64,256]{3,2,1,0:T(8,128)S(1)}, f32[2,64,256]{2,1,0:T(8,128)S(1)}) custom-call(f32[2,8,32,128]{3,2,1,0:T(8,128)} %bitcast.4, bf16[128,256]{1,0:T(8,128)(2,1)} %constant.6.clone.hx_hbm, bf16[256,256]{1,0:T(8,128)(2,1)} %constant.7.clone.hy_hbm, f32[1,128]{1,0:T(1,128)} %bitcast.5, f32[1,128]{1,0:T(1,128)} %bitcast.6, f32[1,64]{1,0:T(1,128)} %bitcast.7), custom_call_target="tpu_custom_call" | custom-call | tf_op jit(solution)/shard_map/pallas_call | solution.py:229
  17.6 0.0 copy-done
  17.6 1.1 %shard_map.74 = f32[2,8,64,64]{3,2,1,0:T(8,128)} custom-call(f32[2,2,64,256]{3,2,1,0:T(8,128)S(1)} %get-tuple-element.7.lines, f32[2,64,256]{2,1,0:T(8,128)S(1)} %get-tuple-element.8.scale, bf16[2,256,256]{2,1,0:T(8,128)(2,1)S(1)} %copy-done), custom_call_target="tpu_custom_call" | custom-call | tf_op jit(solution)/shard_map/pallas_call | solution.py:261
Async XLA Ops:
  0.0 17.6 %copy-start = (bf16[2,256,256]{2,1,0:T(8,128)(2,1)S(1)}, bf16[2,256,256]{2,1,0:T(8,128)(2,1)}, u32[]{:S(2)}) copy-start(bf16[2,256,256]{2,1,0:T(8,128)(2,1)} %constant.8.clone.wz) | copy-start | bytes 786436
